TPU v7x, 256 devices: a whole 4x4x8 slice. The times are simulated.
256 devices in a mesh: dp: 64 (over z_lo, x, y), mp: 4 (over z_hi, core).
Axes of the slice: x: 4, y: 4, z: 8 (z_hi: 2, z_lo: 4; z = z_hi * 4 + z_lo), core: 2. Of those that a mesh axis runs over, the one named last changes fastest.
Arguments:
- features: bfloat16 [16384, 7168], P('dp', 'mp'), may hold values from -6 to 6
- projection: bfloat16 [7168, 256], replicated, may hold values from -0.375 to 0.375
- out_grad: bfloat16 [16384, 20480], P('dp', 'mp'), may hold values from -64 to 64
- momentum: float32 [7168, 20480], P('dp', 'mp'), may hold values from -2 to 2
Outputs:
- new_momentum: float32 [7168, 20480], P('dp', 'mp')
All inputs are finite; a program needn't handle non-finite values.
Results may differ from a plain program's by a relative error of at most 0.0011.
Values may be sent and summed in bfloat16 or wider, within the bound.
A program may use at most 64 MiB of HBM per device.

v0:
```python
import math

import jax
import jax.numpy as jnp
from jax import lax
from jax.sharding import Mesh
from jax.sharding import PartitionSpec as P

FF = 20480
R = 256
MP = ("mp_0", "mp_1")
DP = ("dp_0", "dp_1", "dp_2")
DP_MP = ("dp_0", "dp_1", "dp_2", "mp_0", "mp_1")


def over_axes(shard, axes):
    for axis in axes:
        shard = lax.psum(shard, axis)
    return shard


def local(features, projection, out_grad, momentum):
    mixed_sum = jnp.dot(
        lax.all_gather(features, MP, axis=1, tiled=True),
        projection,
        preferred_element_type=jnp.float32,
    )
    mixed_rows = mixed_sum.astype(jnp.bfloat16)
    norm_level = math.sqrt(R * FF)
    panel_part = lax.psum_scatter(
        lax.dot_general(
            out_grad, mixed_rows, (((0,), (0,)), ((), ())), preferred_element_type=jnp.float32
        ),
        DP,
        scatter_dimension=0,
        tiled=True,
    )
    square_sum = over_axes(jnp.sum(panel_part * panel_part), DP_MP)
    strip_cols = lax.dot_general(
        projection.astype(jnp.float32),
        panel_part,
        (((1,), (1,)), ((), ())),
        precision=lax.Precision.HIGHEST,
        preferred_element_type=jnp.float32,
    )
    decoded = lax.all_to_all(strip_cols, DP, split_axis=0, concat_axis=1, tiled=True)
    factor = jnp.float32(norm_level) / jnp.sqrt(square_sum + 1e-06)
    return 0.9 * momentum + 0.1 * factor * decoded


def solution(mesh):
    finer = Mesh(mesh.devices.reshape(4, 4, 4, 2, 2), ("dp_0", "dp_1", "dp_2", "mp_0", "mp_1"))
    return jax.shard_map(
        local,
        mesh=finer,
        in_specs=(P(DP, MP), P(), P(DP, MP), P(DP, MP)),
        out_specs=P(DP, MP),
        check_vma=False,
    )
```

profile of v0, /device:TPU:1, one launch (start us, length us, event | category | flops | bytes accessed | tf_op | source)
XLA Modules:
  0.0 574.2 jit_solution(7158033960608682947)
XLA Ops:
  6.5 0.0 copy-start
  6.5 0.0 all-gather.2.cloned.1.call-start
  6.5 0.7 all-gather.2.cloned.1.call-update
  7.3 0.0 reduce-scatter.4.cloned.1.call-start
  7.3 66.8 %all-gather.2.cloned.1.call-done = bf16[256,7168]{1,0:T(8,128)(2,1)} async-done(((bf16[256,1792]{1,0:T(8,128)(2,1)}), bf16[256,7168]{1,0:T(8,128)(2,1)}) %all-gather.2.cloned.1.call-update) | async-done | bytes 3670032 | tf_op jit(solution)/shard_map/all_gather | solution.py:24
  74.1 0.0 copy-done
  74.1 8.8 %convolution_bitcast_fusion.1 = f32[5120,256]{0,1:T(8,128)} fusion(bf16[256,5120]{1,0:T(8,128)(2,1)S(1)} %copy-done, bf16[256,7168]{1,0:T(8,128)(2,1)} %all-gather.2.cloned.1.call-done, bf16[7168,256]{1,0:T(8,128)(2,1)} %param.5), kind=kOutput, calls=%fused_computation.1 | convolution fusion | flops 1610678272 | bytes 15204352 | tf_op jit(solution)/shard_map/dot_general | solution.py:31
  82.8 6.0 %copy.14 = f32[5120,256]{1,0:T(8,128)} copy(f32[5120,256]{0,1:T(8,128)} %convolution_bitcast_fusion.1) | data formatting | bytes 10485760
  88.8 0.0 reduce-scatter.4.cloned.1.call-update
  88.8 331.9 %reduce-scatter.4.cloned.1.call-done = f32[80,256]{1,0:T(8,128)} async-done(((f32[5120,256]{1,0:T(8,128)}), f32[80,256]{1,0:T(8,128)}) %reduce-scatter.4.cloned.1.call-update) | async-done | bytes 81936
  420.7 6.9 %convolution_bitcast_fusion = f32[7168,80]{0,1:T(8,128)} fusion(f32[80,256]{1,0:T(8,128)} %reduce-scatter.4.cloned.1.call-done, bf16[7168,256]{1,0:T(8,128)(2,1)} %param.5), kind=kOutput, calls=%fused_computation | convolution fusion | flops 1761607680 | bytes 6045696 | tf_op jit(solution)/shard_map/dot_general | solution.py:39
  427.6 3.8 all_to_all.10
  431.4 4.8 copy.12
  436.2 0.0 copy-start.1
  436.2 5.7 all-to-all-start
  441.9 0.0 copy-done.1
  441.9 0.1 copy.15
  442.0 0.6 multiply_reduce_fusion
  442.6 27.8 %psum.35 = f32[]{:T(128)} all-reduce(f32[]{:T(128)} %multiply_reduce_fusion), channel_id=1, replica_groups=mesh['dp_0'=4,'dp_1'=4,'dp_2'=4,'mp_0'=2,'mp_1'=2] {'dp_0'}, use_global_device_ids=true, to_apply=%region_2.0 | all-reduce | flops 1 | bytes 8 | tf_op jit(solution)/shard_map/psum | solution.py:18
  470.4 6.9 %psum.36 = f32[]{:T(128)} all-reduce(f32[]{:T(128)} %psum.35), channel_id=1, replica_groups=mesh['dp_0'=4,'dp_1'=4,'dp_2'=4,'mp_0'=2,'mp_1'=2] {'dp_1'}, use_global_device_ids=true, to_apply=%region_3.0 | all-reduce | flops 1 | bytes 8 | tf_op jit(solution)/shard_map/psum | solution.py:18
  477.3 9.9 %psum.37 = f32[]{:T(128)} all-reduce(f32[]{:T(128)} %psum.36), channel_id=1, replica_groups=mesh['dp_0'=4,'dp_1'=4,'dp_2'=4,'mp_0'=2,'mp_1'=2] {'dp_2'}, use_global_device_ids=true, to_apply=%region_4.0 | all-reduce | flops 1 | bytes 8 | tf_op jit(solution)/shard_map/psum | solution.py:18
  487.2 8.3 %psum.38 = f32[]{:T(128)} all-reduce(f32[]{:T(128)} %psum.37), channel_id=1, replica_groups=mesh['dp_0'=4,'dp_1'=4,'dp_2'=4,'mp_0'=2,'mp_1'=2] {'mp_0'}, use_global_device_ids=true, to_apply=%region_5.0 | all-reduce | flops 1 | bytes 8 | tf_op jit(solution)/shard_map/psum | solution.py:18
  495.5 60.5 %psum.39 = f32[]{:T(128)} all-reduce(f32[]{:T(128)} %psum.38), channel_id=1, replica_groups=mesh['dp_0'=4,'dp_1'=4,'dp_2'=4,'mp_0'=2,'mp_1'=2] {'mp_1'}, use_global_device_ids=true, to_apply=%region_6.0 | all-reduce | flops 1 | bytes 8 | tf_op jit(solution)/shard_map/psum | solution.py:18
  556.8 0.0 all-to-all-done
  556.8 3.4 broadcast_multiply_fusion
  560.2 3.1 copy.13
  563.3 4.0 multiply_add_fusion
Async XLA Ops:
  6.5 67.5 %copy-start = (bf16[256,5120]{1,0:T(8,128)(2,1)S(1)}, bf16[256,5120]{1,0:T(8,128)(2,1)}, u32[]{:S(2)}) copy-start(bf16[256,5120]{1,0:T(8,128)(2,1)} %param.6) | copy-start | bytes 7864324
  6.5 67.5 %all-gather.2.cloned.1.call-start = ((), (), s32[]{:S(2)}) async-start(), calls=%async_computation.2 | async-start | bytes 4587520 | tf_op jit(solution)/shard_map/all_gather | solution.py:24
  7.3 413.4 %reduce-scatter.4.cloned.1.call-start = ((), (), s32[]{:S(2)}) async-start(), calls=%async_computation.3 | async-start | bytes 5324800
  436.2 5.7 copy-start.1
  436.2 120.6 %all-to-all-start = ((f32[64,112,80]{1,2,0:T(8,128)}), f32[64,112,80]{1,2,0:T(8,128)}, u32[]{:S(2)}, u32[]{:S(2)}) async-start(f32[64,112,80]{1,2,0:T(8,128)} %copy.12), calls=%async_computation | async-start | bytes 5242880 | tf_op jit(solution)/shard_map/all_to_all | solution.py:46
Sparse Core Ops, SparseCore 0:
  9.1 64.8 all-gather.1
  88.9 331.7 reduce-scatter.3
where the time goes:
time: 578 us; the launch traced here: 574 us
  waiting for transfers between devices  399 us (69%)
  blocking collectives  113 us (20%)
  local copies, waits for them, and re-layouts  17.7 us (3%)
  matrix products  15.7 us (3%)
  between operations  14.1 us (2%)
  other arithmetic  8.07 us (1%)
    unnamed x3, waiting for transfers between devices  333 us
    psum x5, blocking collectives, over_axes(): shard = lax.psum(shard, axis)  113 us
    all_gather x1, waiting for transfers between devices, local(): lax.all_gather(features, MP, axis=1, tiled=True)  66.8 us
  transfers between devices with their start and end apart: 3, of which 2 were waited for; matrix products, arithmetic and copies ran while one was open for 0% of the time, Pallas kernels for 0%

commit v1 on v0

v1 whole, which is shorter than its diff:
```python
import math

import jax
import jax.numpy as jnp
from jax import lax
from jax.experimental import pallas as pl
from jax.experimental.pallas import tpu as pltpu
from jax.sharding import Mesh
from jax.sharding import PartitionSpec as P

MESH = pl.DeviceIdType.MESH
D = 7168
FF = 20480
R = 256
TOK = 256
KF = 1792
ROWS = 112
CH = 640
HALF = 2560
WIRE = jnp.float32

MP = ("zh", "c")
DP = ("zl", "x", "y")
PEERS = ("x", "y", "zl")


def dot(a, b):
    return jnp.dot(a, b, preferred_element_type=jnp.float32)


def tile_squares(v):
    rows, cols = v.shape
    total = jnp.zeros((8, 128), jnp.float32)
    for i in range(rows // 8):
        for j in range(cols // 128):
            part = v[8 * i : 8 * i + 8, 128 * j : 128 * j + 128]
            total = total + part * part
    return total


def kernel(
    f_hbm, p_hbm, g_hbm, m_hbm, out_ref,
    f_v, p_v, g_v, mom_v, pd_v,
    mpart, mrecv, msum, mixed, mixed_own,
    panel, crecv, quart, drecv, full,
    dec_s, dec_r, sq,
    load_sem, g_ss, g_rs, m_ss, m_rs, x_ss, x_rs, fw_ss, fw_rs,
    c_ss, c_rs, d_ss, d_rs, e_ss, e_rs, h_ss, h_rs, o_ss, o_rs, q_ss, q_rs,
):
    pos = {a: lax.axis_index(a) for a in ("zl", "x", "y", "zh", "c")}
    sent = []

    def aligned(i, n):
        return pl.multiple_of(i * n, n)

    def send(src, dst, ss, rs, axis, where):
        copy = pltpu.make_async_remote_copy(
            src_ref=src, dst_ref=dst, send_sem=ss, recv_sem=rs,
            device_id={axis: where}, device_id_type=MESH,
        )
        copy.start()
        sent.append(copy)
        return copy

    def ahead(axis, d):
        return lax.rem(pos[axis] + d, 4)

    other = {"zh": 1 - pos["zh"], "c": 1 - pos["c"]}

    loads = {}

    def load(name, src, dst):
        copy = pltpu.make_async_copy(src, dst, load_sem.at[len(loads)])
        copy.start()
        loads[name] = copy

    mp = pos["zh"] * 2 + pos["c"]
    load("f", f_hbm, f_v)
    load("p", p_hbm.at[pl.ds(aligned(mp, KF), KF), :], p_v)
    sets = ("x", "y")
    for s, axis in enumerate(sets):
        load(("g", s), g_hbm.at[:, pl.ds(pl.multiple_of(s * HALF + pos[axis] * CH, 128), CH)], g_v.at[s, 0])
    base = pos["zl"] * 16
    for d in range(4):
        row = base + ahead("x", d) * 4 + pos["y"]
        load(("p", 0, d), p_hbm.at[pl.ds(aligned(row, ROWS), ROWS), :], pd_v.at[0, d])
        row = base + pos["x"] * 4 + ahead("y", d)
        load(("p", 1, d), p_hbm.at[pl.ds(aligned(row, ROWS), ROWS), :], pd_v.at[1, d])
    load("m", m_hbm, mom_v)

    barrier = pltpu.get_barrier_semaphore()
    for axis in PEERS:
        for d in (1, 2, 3):
            pl.semaphore_signal(barrier, inc=1, device_id={axis: ahead(axis, d)}, device_id_type=MESH)
    for axis in ("zh", "c"):
        pl.semaphore_signal(barrier, inc=1, device_id={axis: other[axis]}, device_id_type=MESH)

    loads["f"].wait()
    loads["p"].wait()
    mpart[...] = dot(f_v[...], p_v[...])

    pl.semaphore_wait(barrier, 11)

    mine = pl.ds(aligned(pos["c"], 128), 128)
    theirs = pl.ds(aligned(other["c"], 128), 128)
    m1 = send(mpart.at[theirs, :], mrecv.at[0], m_ss.at[0], m_rs.at[0], "c", other["c"])

    got = {}
    for d in (2, 1, 3):
        for s, axis in enumerate(sets):
            peer = ahead(axis, d)
            got[s, 4 - d] = send(
                g_hbm.at[:, pl.ds(pl.multiple_of(s * HALF + peer * CH, 128), CH)],
                g_v.at[s, 4 - d], g_ss.at[s, d], g_rs.at[s, 4 - d], axis, peer,
            )

    m1.wait_recv()
    msum[...] = mpart[mine, :] + mrecv[0]
    m2 = send(msum, mrecv.at[1], m_ss.at[1], m_rs.at[1], "zh", other["zh"])
    m2.wait_recv()
    mixed_own[:, mine] = (msum[...] + mrecv[1]).T.astype(jnp.bfloat16)
    own = send(mixed_own.at[:, mine], mixed_own.at[:, mine], m_ss.at[2], m_rs.at[2], "c", other["c"])
    direct = {}
    for d in (2, 1, 3):
        for s, axis in enumerate(sets):
            direct[s, 4 - d] = send(
                mixed_own.at[:, mine], mixed.at[s, 4 - d, :, mine],
                x_ss.at[s, d], x_rs.at[s, 4 - d], axis, ahead(axis, d),
            )
    passed = {}
    order = [(s, k) for k in (1, 3, 2) for s in (0, 1)]
    for s, k in order:
        direct[s, k].wait_recv()
        passed[s, k] = send(
            mixed.at[s, k, :, mine], mixed.at[s, k, :, mine],
            fw_ss.at[s, k], fw_rs.at[s, k], "c", other["c"],
        )

    own.wait_recv()
    for s in (0, 1):
        loads["g", s].wait()
        panel[s] = dot(mixed_own[...], g_v[s, 0])
    for s, k in order:
        passed[s, k].wait_recv()
        got[s, k].wait_recv()
        panel[s] += dot(mixed[s, k], g_v[s, k])

    cross = ("y", "x")
    arrived = {}
    for d in (2, 1, 3):
        for s, axis in enumerate(cross):
            peer = ahead(axis, d)
            arrived[s, d] = send(
                panel.at[s, pl.ds(aligned(peer, 64), 64), :], crecv.at[s, d - 1],
                c_ss.at[s, d], c_rs.at[s, d], axis, peer,
            )
    for s, axis in enumerate(cross):
        for d in (1, 2, 3):
            arrived[s, d].wait_recv()
        quart[s] = (panel[s, pl.ds(aligned(pos[axis], 64), 64), :] + crecv[s, 0]) + (crecv[s, 1] + crecv[s, 2])
    arrived = {}
    for d in (3, 2, 1):
        for s in (0, 1):
            peer = ahead("zl", d)
            arrived[s, d] = send(
                quart.at[s, pl.ds(aligned(peer, 16), 16), :], drecv.at[s, d - 1],
                d_ss.at[s, d], d_rs.at[s, d], "zl", peer,
            )
    squares = jnp.zeros((8, 128), jnp.float32)
    pieces = []
    for s, axis in enumerate(cross):
        for d in (1, 2, 3):
            arrived[s, d].wait_recv()
        total = (quart[s, pl.ds(aligned(pos["zl"], 16), 16), :] + drecv[s, 0]) + (drecv[s, 1] + drecv[s, 2])
        piece = pl.ds(pl.multiple_of(pos[axis] * 64 + pos["zl"] * 16, 16), 16)
        full[s, piece, :] = total
        pieces.append(piece)
        squares = squares + tile_squares(total)

    sq[0, 0] = squares

    def spread(level, axis):
        return [send(sq.at[level, 0], sq.at[level, d], q_ss.at[level, d], q_rs.at[level, d], axis, ahead(axis, d)) for d in (1, 2, 3)]

    def collect(level, copies):
        for copy in copies:
            copy.wait_recv()
        sq[level + 1, 0] = (sq[level, 0] + sq[level, 1]) + (sq[level, 2] + sq[level, 3])

    def pair(level, axis):
        return send(sq.at[level, 0], sq.at[level, 1], q_ss.at[level, 1], q_rs.at[level, 1], axis, other[axis])

    arrived = {}
    for d in (3, 2, 1):
        for s in (0, 1):
            arrived[s, d] = send(
                full.at[s, pieces[s], :], full.at[s, pieces[s], :],
                e_ss.at[s, d], e_rs.at[s, d], "zl", ahead("zl", d),
            )
    q = spread(0, "zl")
    for s in (0, 1):
        for d in (1, 2, 3):
            arrived[s, d].wait_recv()
    arrived = {}
    for d in (2, 1, 3):
        for s, axis in enumerate(cross):
            block = pl.ds(aligned(pos[axis], 64), 64)
            arrived[s, d] = send(
                full.at[s, block, :], full.at[s, block, :],
                h_ss.at[s, d], h_rs.at[s, d], axis, ahead(axis, d),
            )
    collect(0, q)
    q = spread(1, "y")
    collect(1, q)
    q = spread(2, "x")
    for s in (0, 1):
        for d in (1, 2, 3):
            arrived[s, d].wait_recv()

    final = {}
    for s, axis in enumerate(sets):
        whole = full[s]
        high = whole.astype(jnp.bfloat16)
        low = (whole - high.astype(jnp.float32)).astype(jnp.bfloat16)
        for d in (2, 1, 3, 0):
            loads["p", s, d].wait()
            rows = dot(pd_v[s, d], high) + dot(pd_v[s, d], low)
            if d == 0:
                dec_r[s, 0] = rows.astype(WIRE)
            else:
                dec_s[s, d - 1] = rows.astype(WIRE)
                final[s, 4 - d] = send(
                    dec_s.at[s, d - 1], dec_r.at[s, 4 - d],
                    o_ss.at[s, d], o_rs.at[s, 4 - d], axis, ahead(axis, d),
                )
    collect(2, q)
    p = pair(3, "c")
    p.wait_recv()
    sq[4, 0] = sq[3, 0] + sq[3, 1]
    p = pair(4, "zh")
    p.wait_recv()
    square_sum = jnp.sum(sq[4, 0] + sq[4, 1], axis=(0, 1), keepdims=True)
    scale = 0.1 * (jnp.float32(math.sqrt(R * FF)) / jnp.sqrt(square_sum + 1e-06))

    loads["m"].wait()
    for k in (0, 1, 3, 2):
        for s, axis in enumerate(sets):
            if k:
                final[s, k].wait_recv()
            cols = pl.ds(pl.multiple_of(s * HALF + ahead(axis, k) * CH, 128), CH)
            out_ref[:, cols] = 0.9 * mom_v[:, cols] + scale * dec_r[s, k].astype(jnp.float32)
    for copy in sent:
        copy.wait_send()


def local(features, projection, out_grad, momentum):
    dma = pltpu.SemaphoreType.DMA
    f32, bf16 = jnp.float32, jnp.bfloat16
    return pl.pallas_call(
        kernel,
        out_shape=jax.ShapeDtypeStruct((ROWS, 2 * HALF), f32),
        in_specs=[pl.BlockSpec(memory_space=pl.ANY)] * 4,
        out_specs=pl.BlockSpec(memory_space=pltpu.VMEM),
        scratch_shapes=[
            pltpu.VMEM((TOK, KF), bf16),
            pltpu.VMEM((KF, R), bf16),
            pltpu.VMEM((2, 4, TOK, CH), bf16),
            pltpu.VMEM((ROWS, 2 * HALF), f32),
            pltpu.VMEM((2, 4, ROWS, R), bf16),
            pltpu.VMEM((TOK, R), f32),
            pltpu.VMEM((2, 128, R), f32),
            pltpu.VMEM((128, R), f32),
            pltpu.VMEM((2, 4, R, TOK), bf16),
            pltpu.VMEM((R, TOK), bf16),
            pltpu.VMEM((2, R, CH), f32),
            pltpu.VMEM((2, 3, 64, CH), f32),
            pltpu.VMEM((2, 64, CH), f32),
            pltpu.VMEM((2, 3, 16, CH), f32),
            pltpu.VMEM((2, R, CH), f32),
            pltpu.VMEM((2, 3, ROWS, CH), WIRE),
            pltpu.VMEM((2, 4, ROWS, CH), WIRE),
            pltpu.VMEM((5, 4, 8, 128), f32),
            dma((16,)),
            dma((2, 4)), dma((2, 4)),
            dma((3,)), dma((3,)),
            dma((2, 4)), dma((2, 4)),
            dma((2, 4)), dma((2, 4)),
            dma((2, 4)), dma((2, 4)),
            dma((2, 4)), dma((2, 4)),
            dma((2, 4)), dma((2, 4)),
            dma((2, 4)), dma((2, 4)),
            dma((2, 4)), dma((2, 4)),
            dma((5, 4)), dma((5, 4)),
        ],
        compiler_params=pltpu.CompilerParams(
            collective_id=0, has_side_effects=True, vmem_limit_bytes=40 * 1024 * 1024,
        ),
        name="flora",
    )(features, projection, out_grad, momentum)


def solution(mesh):
    finer = Mesh(mesh.devices.reshape(4, 4, 4, 2, 2), ("zl", "x", "y", "zh", "c"))
    return jax.shard_map(
        local,
        mesh=finer,
        in_specs=(P(DP, MP), P(), P(DP, MP), P(DP, MP)),
        out_specs=P(DP, MP),
        check_vma=False,
    )
```

time: 578 us -> 96.6 us (0.17)
  waiting for transfers between devices: 399 us -> 0 us
  blocking collectives: 113 us -> 0 us
  Pallas kernels: 0 us -> 88.4 us
  matrix products: 15.7 us -> 0 us
  between operations: 14.1 us -> 0.01 us
  local copies, waits for them, and re-layouts: 17.7 us -> 7.99 us
  other arithmetic: 8.07 us -> 0 us
    unnamed x3 -> x0, waiting for transfers between devices: 333 us -> none
    psum x5 -> x0, blocking collectives: 113 us -> none  [over_axes(): shard = lax.psum(shard, axis)]
    pallas_call x0 -> x1, Pallas kernels: none -> 88.4 us  [local(): pl.pallas_call(kernel, out_shape=jax.ShapeDtypeStruct((ROWS, 2 * HALF), f...]
    all_gather x1 -> x0, waiting for transfers between devices: 66.8 us -> none  [local(): lax.all_gather(features, MP, axis=1, tiled=True)]
    dot_general x2 -> x0, matrix products: 15.7 us -> none  [the longest x1 8.76 us: local(): lax.dot_general(out_grad, mixed_rows, (((0,), (0,)), ((), ())), preferred...]
    all_to_all x2 -> x0, local copies, waits for them, and re-layouts: 8.55 us -> none  [local(): lax.all_to_all(strip_cols, DP, split_axis=0, concat_axis=1, tiled=True)]
  transfers between devices with their start and end apart: 3 -> 0, of which waited for: 2 -> 0; matrix products, arithmetic and copies ran while one was open for 0% -> 0% of each run, Pallas kernels for 0% -> 0%
where the time goes in v1:
time: 96.6 us; the launch traced here: 96.4 us
  Pallas kernels  88.4 us (92%)
  local copies, waits for them, and re-layouts  7.99 us (8%)
    pallas_call x1, Pallas kernels, local(): pl.pallas_call(kernel, out_shape=jax.ShapeDtypeStruct((ROWS, 2 * HALF), f...  88.4 us
    unnamed x9, local copies, waits for them, and re-layouts  7.99 us

profile of v1, /device:TPU:1, one launch (start us, length us, event | category | flops | bytes accessed | tf_op | source)
XLA Modules:
  0.0 96.4 jit_solution(9807804779151262638)
XLA Ops:
  0.0 0.0 copy-start
  0.0 2.0 %copy-done = bf16[7168,256]{1,0:T(8,128)(2,1)S(1)} copy-done((bf16[7168,256]{1,0:T(8,128)(2,1)S(1)}, bf16[7168,256]{1,0:T(8,128)(2,1)}, u32[]{:S(2)}) %copy-start) | copy-done | bytes 3670040
  2.0 0.0 copy-start.1
  2.0 1.7 %copy-done.1 = bf16[256,5120]{1,0:T(8,128)(2,1)S(1)} copy-done((bf16[256,5120]{1,0:T(8,128)(2,1)S(1)}, bf16[256,5120]{1,0:T(8,128)(2,1)}, u32[]{:S(2)}) %copy-start.1) | copy-done | bytes 2621464
  3.8 0.0 copy-start.2
  3.8 1.6 %copy-done.2 = f32[112,5120]{1,0:T(8,128)S(1)} copy-done((f32[112,5120]{1,0:T(8,128)S(1)}, f32[112,5120]{1,0:T(8,128)}, u32[]{:S(2)}) %copy-start.2) | copy-done | bytes 2293784
  5.4 0.0 copy-start.3
  5.4 1.2 %copy-done.3 = bf16[256,1792]{1,0:T(8,128)(2,1)S(1)} copy-done((bf16[256,1792]{1,0:T(8,128)(2,1)S(1)}, bf16[256,1792]{1,0:T(8,128)(2,1)}, u32[]{:S(2)}) %copy-start.3) | copy-done | bytes 917528
  6.6 88.4 %flora.1 = f32[112,5120]{1,0:T(8,128)S(1)} custom-call(bf16[256,1792]{1,0:T(8,128)(2,1)S(1)} %copy-done.3, bf16[7168,256]{1,0:T(8,128)(2,1)S(1)} %copy-done, bf16[256,5120]{1,0:T(8,128)(2,1)S(1)} %copy-done.1, f32[112,5120]{1,0:T(8,128)S(1)} %copy-done.2), custom_call_target="tpu_custom_call" | custom-call | tf_op jit(solution)/shard_map/flora/pallas_call | solution.py:259
  95.0 1.4 %copy.6 = f32[112,5120]{1,0:T(8,128)} copy(f32[112,5120]{1,0:T(8,128)S(1)} %flora.1) | data formatting | bytes 4587520
Async XLA Ops:
  0.0 2.0 %copy-start = (bf16[7168,256]{1,0:T(8,128)(2,1)S(1)}, bf16[7168,256]{1,0:T(8,128)(2,1)}, u32[]{:S(2)}) copy-start(bf16[7168,256]{1,0:T(8,128)(2,1)} %p_hbm.1) | copy-start | bytes 11010052
  2.0 1.7 %copy-start.1 = (bf16[256,5120]{1,0:T(8,128)(2,1)S(1)}, bf16[256,5120]{1,0:T(8,128)(2,1)}, u32[]{:S(2)}) copy-start(bf16[256,5120]{1,0:T(8,128)(2,1)} %g_hbm.1) | copy-start | bytes 7864324
  3.8 1.6 %copy-start.2 = (f32[112,5120]{1,0:T(8,128)S(1)}, f32[112,5120]{1,0:T(8,128)}, u32[]{:S(2)}) copy-start(f32[112,5120]{1,0:T(8,128)} %m_hbm.1) | copy-start | bytes 6881284
  5.4 1.2 %copy-start.3 = (bf16[256,1792]{1,0:T(8,128)(2,1)S(1)}, bf16[256,1792]{1,0:T(8,128)(2,1)}, u32[]{:S(2)}) copy-start(bf16[256,1792]{1,0:T(8,128)(2,1)} %f_hbm.1) | copy-start | bytes 2752516

commit v2 on v0

v2 whole, which is shorter than its diff:
```python
import math

import jax
import jax.numpy as jnp
from jax import lax
from jax.experimental import pallas as pl
from jax.experimental.pallas import tpu as pltpu
from jax.sharding import Mesh
from jax.sharding import PartitionSpec as P

MESH = pl.DeviceIdType.MESH
FF = 20480
R = 256
TOK = 256
KF = 1792
ROWS = 112
CH = 640
HALF = 2560
BATCHES = ((0, 384), (384, 256))
C_TYPE = jnp.bfloat16
E_TYPE = jnp.bfloat16
G_TYPE = jnp.bfloat16
EARLY = 1
SEMS = 16 + 6 * len(BATCHES)

MP = ("zh", "c")
DP = ("zl", "x", "y")
RING = ("x", "y")
CROSS = ("y", "x")
BOTH = (0, 1)


def dot(a, b):
    return jnp.dot(a, b, preferred_element_type=jnp.float32)


def tile_squares(v):
    rows, cols = v.shape
    total = jnp.zeros((8, 128), jnp.float32)
    for i in range(rows // 8):
        for j in range(cols // 128):
            part = v[8 * i : 8 * i + 8, 128 * j : 128 * j + 128]
            total = total + part * part
    return total


def kernel(
    f_hbm, p_hbm, g_hbm, m_hbm, out_ref,
    f_v, p_v, g_v, mom_v, pd_v,
    mpart, mrecv, msum, mixed,
    panel, panel_s, crecv, quart, drecv, full,
    dec_s, dec_r, sq,
    load_sem, ss, rs,
):
    pos = {a: lax.axis_index(a) for a in ("zl", "x", "y", "zh", "c")}
    other = {"zh": 1 - pos["zh"], "c": 1 - pos["c"]}
    groups = []
    scope = jax.named_scope

    def aligned(i, n):
        return pl.multiple_of(i * n, n)

    def ahead(axis, d):
        return lax.rem(pos[axis] + d, 4)

    def remote(src, dst, i, where):
        return pltpu.make_async_remote_copy(
            src_ref=src, dst_ref=dst, send_sem=ss.at[i], recv_sem=rs.at[i],
            device_id=where, device_id_type=MESH,
        )

    def send(copies, whole):
        i = len(groups)
        for src, dst, where in copies:
            remote(src, dst, i, where).start()
        group = remote(whole, whole, i, copies[0][2])
        groups.append(group)
        return group

    barrier = pltpu.get_barrier_semaphore()
    z_peers = [{"zl": ahead("zl", d)} for d in (1, 2, 3)]
    z_peers += [{"zl": ahead("zl", d), "zh": other["zh"]} for d in (1, 2, 3)] + [{"zh": other["zh"]}]
    greeted = [{axis: ahead(axis, d)} for axis in RING for d in (1, 2, 3)] + z_peers + [{"c": other["c"]}]
    for where in greeted:
        pl.semaphore_signal(barrier, inc=1, device_id=where, device_id_type=MESH)

    loads = {}

    def load(name, src, dst):
        copy = pltpu.make_async_copy(src, dst, load_sem.at[len(loads)])
        copy.start()
        loads[name] = copy

    mp = pos["zh"] * 2 + pos["c"]
    load("f", f_hbm, f_v)
    load("p", p_hbm.at[pl.ds(aligned(mp, KF), KF), :], p_v)

    def late_loads():
        for s in BOTH:
            first = pl.multiple_of(s * HALF + pos[RING[s]] * CH, 128)
            load(("g", s), g_hbm.at[:, pl.ds(first, CH)], g_v.at[s, pl.ds(0, TOK), :])
        base = pos["zl"] * 16
        for d in range(4):
            row = base + ahead("x", d) * 4 + pos["y"]
            load(("p", 0, d), p_hbm.at[pl.ds(aligned(row, ROWS), ROWS), :], pd_v.at[0, pl.ds(d * ROWS, ROWS), :])
            row = base + pos["x"] * 4 + ahead("y", d)
            load(("p", 1, d), p_hbm.at[pl.ds(aligned(row, ROWS), ROWS), :], pd_v.at[1, pl.ds(d * ROWS, ROWS), :])
        load("m", m_hbm, mom_v)

    mine = pl.ds(aligned(pos["c"], 128), 128)
    theirs = pl.ds(aligned(other["c"], 128), 128)
    ring_order = (2, 1, 3)

    def lanes(b):
        off, width = BATCHES[b]
        return pl.ds(off, width)

    def grad_send(b):
        off, width = BATCHES[b]
        copies = []
        for d in ring_order:
            for s, axis in enumerate(RING):
                peer = ahead(axis, d)
                first = pl.multiple_of(s * HALF + peer * CH + off, 128)
                copies.append((
                    g_hbm.at[:, pl.ds(first, width)], g_v.at[s, pl.ds(d * TOK, TOK), lanes(b)], {axis: peer}
                ))
        return send(copies, g_v.at[:, pl.ds(TOK, 3 * TOK), lanes(b)])

    def sum_send(b):
        cols = lanes(b)
        for s in BOTH:
            panel[s, :, cols] = dot(mixed[s], g_v[s, :, cols])
        source = panel
        if C_TYPE != jnp.float32:
            source = panel_s
            panel_s[:, :, cols] = panel[:, :, cols].astype(C_TYPE)
        copies = []
        for d in ring_order:
            for s, axis in enumerate(CROSS):
                peer = ahead(axis, d)
                copies.append((
                    source.at[s, pl.ds(aligned(peer, 64), 64), cols], crecv.at[s, d - 1, :, cols], {axis: peer}
                ))
        return send(copies, crecv.at[:, :, :, cols])

    half, odd = lax.div(pos["zl"], 2), lax.rem(pos["zl"], 2)
    z_to = (3 - 3 * half, 2 - half, pos["zl"] + 1 - 2 * odd)

    def reduce_send(b, group):
        cols = lanes(b)
        with scope(f"C{b}"):
            group.wait_recv()
        for s, axis in enumerate(CROSS):
            total = panel[s, pl.ds(aligned(pos[axis], 64), 64), cols]
            for d in (1, 2, 3):
                total = total + crecv[s, d - 1, :, cols].astype(jnp.float32)
            quart[s, :, cols] = total
        copies = []
        for j, to in enumerate(z_to):
            for s in BOTH:
                slot = odd if j < 2 else 2
                copies.append((quart.at[s, pl.ds(aligned(to, 16), 16), cols], drecv.at[s, slot, :, cols], {"zl": to}))
        return send(copies, drecv.at[:, :, :, cols])

    squares = []

    def gather_send(b, group):
        cols = lanes(b)
        with scope(f"D{b}"):
            group.wait_recv()
        copies = []
        for s in BOTH:
            total = quart[s, pl.ds(aligned(pos["zl"], 16), 16), cols]
            total = (total + drecv[s, 2, :, cols]) + (drecv[s, 0, :, cols] + drecv[s, 1, :, cols])
            place = pl.ds(pl.multiple_of(pos[CROSS[s]] * 64 + pos["zl"] * 16, 16), 16)
            full[s, place, cols] = total.astype(E_TYPE)
            squares.append(tile_squares(total))
            piece = full.at[s, place, cols]
            copies += [(j, s, piece, piece, {"zl": to}) for j, to in enumerate(z_to)]
        copies = [c[2:] for c in sorted(copies, key=lambda c: c[:2])]
        return send(copies, full.at[:, pl.ds(0, 48), cols])

    def cross_send(b, group):
        cols = lanes(b)
        with scope(f"E{b}"):
            group.wait_recv()
        copies = []
        for d in ring_order:
            for s, axis in enumerate(CROSS):
                block = full.at[s, pl.ds(aligned(pos[axis], 64), 64), cols]
                copies.append((block, block, {axis: ahead(axis, d)}))
        return send(copies, full.at[:, pl.ds(0, 192), cols])

    def decode_send(b, group):
        cols = lanes(b)
        with scope(f"F{b}"):
            group.wait_recv()
        if b == 0:
            for s in BOTH:
                for d in range(4):
                    loads["p", s, d].wait()
        for s in BOTH:
            whole = full[s, :, cols]
            if E_TYPE == jnp.float32:
                high = whole.astype(jnp.bfloat16)
                low = (whole - high.astype(jnp.float32)).astype(jnp.bfloat16)
                rows = dot(pd_v[s], high) + dot(pd_v[s], low)
            else:
                rows = dot(pd_v[s], whole)
            panel[s, pl.ds(0, ROWS), cols] = rows[:ROWS]
            for d in (1, 2, 3):
                dec_s[s, d - 1, :, cols] = rows[d * ROWS : (d + 1) * ROWS].astype(G_TYPE)
        copies = []
        for d in ring_order:
            for s, axis in enumerate(RING):
                copies.append((dec_s.at[s, d - 1, :, cols], dec_r.at[s, d - 1, :, cols], {axis: ahead(axis, d)}))
        return send(copies, dec_r.at[:, :, :, cols])

    def spread(level, peers):
        n = len(peers)
        copies = [(sq.at[level, 0], sq.at[level, 1 + k], where) for k, where in enumerate(peers)]
        return send(copies, sq.at[level, pl.ds(1, n)])

    def collect(level, group, n):
        with scope(f"sq{level}"):
            group.wait_recv()
        total = sq[level, 0]
        for k in range(n):
            total = total + sq[level, 1 + k]
        sq[level + 1, 0] = total

    every = range(len(BATCHES))
    with scope("barrier"):
        pl.semaphore_wait(barrier, len(greeted))
    grads = [grad_send(b) for b in every[:EARLY]]
    with scope("mpart"):
        loads["f"].wait()
        loads["p"].wait()
        mpart[...] = dot(f_v[...], p_v[...])
    m1 = send([(mpart.at[theirs, :], mrecv.at[0], {"c": other["c"]})], mrecv.at[0])
    late_loads()
    with scope("m1"):
        m1.wait_recv()
    msum[...] = mpart[mine, :] + mrecv[0]
    m2 = send([(msum, mrecv.at[1], {"zh": other["zh"]})], msum)
    with scope("m2"):
        m2.wait_recv()
    own = (msum[...] + mrecv[1]).T.astype(jnp.bfloat16)
    for s in BOTH:
        mixed[s, :, mine] = own

    def lane_of(d, c):
        return pl.ds(pl.multiple_of(d * TOK + c * 128, 128), 128)

    core = {"c": other["c"]}
    own = mixed.at[0, :, mine]
    direct = {}
    for d in ring_order:
        for s, axis in enumerate(RING):
            there = mixed.at[s, :, lane_of(d, pos["c"])]
            direct[s, d] = send([(own, there, {axis: ahead(axis, d)})], own)
    passed = [send([(mixed.at[s, :, mine], mixed.at[s, :, mine], core) for s in BOTH], mixed.at[:, :, pl.ds(0, 128)])]
    grads += [grad_send(b) for b in every[EARLY:]]
    for d in (1, 3, 2):
        copies = []
        for s in BOTH:
            with scope(f"direct{s}{d}"):
                direct[s, d].wait_recv()
            here = mixed.at[s, :, lane_of(d, pos["c"])]
            copies.append((here, here, core))
        passed.append(send(copies, mixed.at[:, :, pl.ds(d * TOK, 128)]))
    with scope("passed"):
        for group in passed:
            group.wait_recv()
        for s in BOTH:
            loads["g", s].wait()
    moving = []
    for b in every:
        with scope(f"got{b}"):
            grads[b].wait_recv()
        moving.append(sum_send(b))
    moving = [reduce_send(b, moving[b]) for b in every]
    moving = [gather_send(b, moving[b]) for b in every]
    total = squares[0]
    for one in squares[1:]:
        total = total + one
    sq[0, 0] = total
    q = spread(0, [{"y": ahead("y", d)} for d in (1, 2, 3)])
    moving = [cross_send(b, moving[b]) for b in every]
    collect(0, q, 3)
    q = spread(1, [{"x": ahead("x", d)} for d in (1, 2, 3)])
    final = [decode_send(b, moving[b]) for b in every[:-1]]
    collect(1, q, 3)
    q = spread(2, z_peers)
    final.append(decode_send(every[-1], moving[-1]))
    collect(2, q, 7)
    q = spread(3, [core])
    collect(3, q, 1)
    square_sum = jnp.sum(sq[4, 0], axis=(0, 1), keepdims=True)
    scale = 0.1 * (jnp.float32(math.sqrt(R * FF)) / jnp.sqrt(square_sum + 1e-06))

    loads["m"].wait()

    def finish(s, d, off, width, rows):
        origin = lax.rem(pos[RING[s]] + 4 - d, 4)
        cols = pl.ds(pl.multiple_of(s * HALF + origin * CH + off, 128), width)
        out_ref[:, cols] = 0.9 * mom_v[:, cols] + scale * rows.astype(jnp.float32)

    for s in BOTH:
        finish(s, 0, 0, CH, panel[s, pl.ds(0, ROWS), :])
    for b in every:
        with scope(f"fin{b}"):
            final[b].wait_recv()
        for s in BOTH:
            for d in (1, 2, 3):
                finish(s, d, *BATCHES[b], dec_r[s, d - 1, :, lanes(b)])
    with scope("sendwait"):
        for group in groups:
            group.wait_send()


def local(features, projection, out_grad, momentum):
    dma = pltpu.SemaphoreType.DMA
    f32, bf16 = jnp.float32, jnp.bfloat16
    return pl.pallas_call(
        kernel,
        out_shape=jax.ShapeDtypeStruct((ROWS, 2 * HALF), f32),
        in_specs=[pl.BlockSpec(memory_space=pltpu.HBM)] * 4,
        out_specs=pl.BlockSpec(memory_space=pltpu.VMEM),
        scratch_shapes=[
            pltpu.VMEM((TOK, KF), bf16),
            pltpu.VMEM((KF, R), bf16),
            pltpu.VMEM((2, 4 * TOK, CH), bf16),
            pltpu.VMEM((ROWS, 2 * HALF), f32),
            pltpu.VMEM((2, 4 * ROWS, R), bf16),
            pltpu.VMEM((TOK, R), f32),
            pltpu.VMEM((2, 128, R), f32),
            pltpu.VMEM((128, R), f32),
            pltpu.VMEM((2, R, 4 * TOK), bf16),
            pltpu.VMEM((2, R, CH), f32),
            pltpu.VMEM((2, R, CH), C_TYPE),
            pltpu.VMEM((2, 3, 64, CH), C_TYPE),
            pltpu.VMEM((2, 64, CH), f32),
            pltpu.VMEM((2, 3, 16, CH), f32),
            pltpu.VMEM((2, R, CH), E_TYPE),
            pltpu.VMEM((2, 3, ROWS, CH), G_TYPE),
            pltpu.VMEM((2, 3, ROWS, CH), G_TYPE),
            pltpu.VMEM((5, 8, 8, 128), f32),
            dma((13,)),
            dma((SEMS,)),
            dma((SEMS,)),
        ],
        compiler_params=pltpu.CompilerParams(
            collective_id=0, has_side_effects=True, vmem_limit_bytes=40 * 1024 * 1024,
        ),
        name="flora",
    )(*[pltpu.with_memory_space_constraint(a, pltpu.HBM) for a in (features, projection, out_grad, momentum)])


def solution(mesh):
    finer = Mesh(mesh.devices.reshape(4, 4, 4, 2, 2), ("zl", "x", "y", "zh", "c"))
    return jax.shard_map(
        local,
        mesh=finer,
        in_specs=(P(DP, MP), P(), P(DP, MP), P(DP, MP)),
        out_specs=P(DP, MP),
        check_vma=False,
    )
```

time: 578 us -> 60 us (0.10)
  waiting for transfers between devices: 399 us -> 0 us
  blocking collectives: 113 us -> 0 us
  Pallas kernels: 0 us -> 58.5 us
  local copies, waits for them, and re-layouts: 17.7 us -> 1.39 us
  matrix products: 15.7 us -> 0 us
  between operations: 14.1 us -> 0.01 us
  other arithmetic: 8.07 us -> 0 us
    unnamed x3 -> x0, waiting for transfers between devices: 333 us -> none
    psum x5 -> x0, blocking collectives: 113 us -> none  [over_axes(): shard = lax.psum(shard, axis)]
    all_gather x1 -> x0, waiting for transfers between devices: 66.8 us -> none  [local(): lax.all_gather(features, MP, axis=1, tiled=True)]
    pallas_call x0 -> x1, Pallas kernels: none -> 58.5 us  [local(): pl.pallas_call(kernel, out_shape=jax.ShapeDtypeStruct((ROWS, 2 * HALF), f...]
    dot_general x2 -> x0, matrix products: 15.7 us -> none  [the longest x1 8.76 us: local(): lax.dot_general(out_grad, mixed_rows, (((0,), (0,)), ((), ())), preferred...]
    all_to_all x2 -> x0, local copies, waits for them, and re-layouts: 8.55 us -> none  [local(): lax.all_to_all(strip_cols, DP, split_axis=0, concat_axis=1, tiled=True)]
  transfers between devices with their start and end apart: 3 -> 0, of which waited for: 2 -> 0; matrix products, arithmetic and copies ran while one was open for 0% -> 0% of each run, Pallas kernels for 0% -> 0%
where the time goes in v2:
time: 60 us; the launch traced here: 59.9 us
  Pallas kernels  58.5 us (98%)
  local copies, waits for them, and re-layouts  1.39 us (2%)
    pallas_call x1, Pallas kernels, local(): pl.pallas_call(kernel, out_shape=jax.ShapeDtypeStruct((ROWS, 2 * HALF), f...  58.5 us
    unnamed x1, local copies, waits for them, and re-layouts  1.39 us

profile of v2, /device:TPU:1, one launch (start us, length us, event | category | flops | bytes accessed | tf_op | source)
XLA Modules:
  0.0 59.9 jit_solution(9221963314656988653)
XLA Ops:
  0.0 58.5 %flora.1 = f32[112,5120]{1,0:T(8,128)S(1)} custom-call(bf16[256,1792]{1,0:T(8,128)(2,1)} %f_hbm.1, bf16[7168,256]{1,0:T(8,128)(2,1)} %p_hbm.1, bf16[256,5120]{1,0:T(8,128)(2,1)} %g_hbm.1, f32[112,5120]{1,0:T(8,128)} %m_hbm.1), custom_call_target="tpu_custom_call" | custom-call | tf_op jit(solution)/shard_map/flora/pallas_call | solution.py:326
  58.5 1.4 %copy.6 = f32[112,5120]{1,0:T(8,128)} copy(f32[112,5120]{1,0:T(8,128)S(1)} %flora.1) | data formatting | bytes 4587520

commit v3 on v0

v3 whole, which is shorter than its diff:
```python
import math

import jax
import jax.numpy as jnp
from jax import lax
from jax.experimental import pallas as pl
from jax.experimental.pallas import tpu as pltpu
from jax.sharding import Mesh
from jax.sharding import PartitionSpec as P

MESH = pl.DeviceIdType.MESH
FF = 20480
R = 256
TOK = 256
KF = 1792
ROWS = 112
COLS = 5120
CHUNK = (640, 512, 128)
BASE = (0, 2560, 4608)
RING = ("a", "b", "z")
CROSS = ("b", "a", "a")
THIRD = ("z", "z", "b")
BATCHES = (((0, 0, 384), (1, 0, 256)), ((0, 384, 256), (1, 256, 256)), ((2, 0, 128),))
Z = 2
LANES = sum(CHUNK)
C_TYPE = jnp.bfloat16
E_TYPE = jnp.bfloat16
G_TYPE = jnp.bfloat16
AHEAD = 3
SEMS = 16 + 6 * len(BATCHES)

MP = ("zh", "c")
DP = ("zl", "x", "y")
BOTH = (0, 1)


def segments():
    out, lane = [], 0
    for batch in BATCHES:
        out.append([])
        for s, off, width in batch:
            out[-1].append((s, off, width, pl.ds(lane, width)))
            lane += width
    return out


def dot(a, b):
    return jnp.dot(a, b, preferred_element_type=jnp.float32)


def tile_squares(v):
    rows, cols = v.shape
    total = jnp.zeros((8, 128), jnp.float32)
    for i in range(rows // 8):
        for j in range(cols // 128):
            part = v[8 * i : 8 * i + 8, 128 * j : 128 * j + 128]
            total = total + part * part
    return total


def kernel(
    f_hbm, p_hbm, g_hbm, m_hbm, out_ref,
    f_v, p_v, g_v, mom_v, pd_v,
    mpart, mrecv, msum, mixed,
    panel, panel_s, crecv, quart, drecv, full,
    dec_s, dec_r, sq,
    load_sem, ss, rs, ready,
):
    scope = jax.named_scope
    at = {a: lax.axis_index(a) for a in ("zl", "x", "y", "zh", "c")}
    zl, x, y, zh, c = (at[a] for a in ("zl", "x", "y", "zh", "c"))
    core, partner = {"c": 1 - c}, {"zh": 1 - zh}
    pos = {"a": x * (1 - c) + y * c, "b": x * c + y * (1 - c), "z": zl}
    groups = []
    segs = segments()
    every = range(len(BATCHES))

    def aligned(i, n):
        return pl.multiple_of(i * n, n)

    half, odd = lax.div(zl, 2), lax.rem(zl, 2)
    z_to = (3 - 3 * half, 2 - half, zl + 1 - 2 * odd)
    z_from = (2 - 2 * half, 3 - 2 * half, zl + 1 - 2 * odd)

    def step(axis, d):
        on_x = 1 - c if axis == "a" else c
        return {"x": lax.rem(x + d * on_x, 4), "y": lax.rem(y + d * (1 - on_x), 4)}

    peers = {axis: [(lax.rem(pos[axis] + d, 4), step(axis, d), d - 1) for d in (2, 1, 3)] for axis in ("a", "b")}
    peers["z"] = [(to, {"zl": to}, odd if j < 2 else 2) for j, to in enumerate(z_to)]

    def origin(axis, slot):
        return z_from[slot] if axis == "z" else lax.rem(pos[axis] + 3 - slot, 4)

    def remote(src, dst, i, where):
        return pltpu.make_async_remote_copy(
            src_ref=src, dst_ref=dst, send_sem=ss.at[i], recv_sem=rs.at[i],
            device_id=where, device_id_type=MESH,
        )

    def group_of(whole):
        groups.append(remote(whole, whole, len(groups), core))
        return len(groups) - 1

    def start(group, copies):
        for src, dst, where in copies:
            remote(src, dst, group, where).start()

    def send(copies, whole):
        group = group_of(whole)
        start(group, copies)
        return group

    def arrive(name, group):
        with scope(name):
            groups[group].wait_recv()

    def lanes(b):
        first = segs[b][0][3].start
        return pl.ds(first, sum(width for _, _, width, _ in segs[b]))

    barrier = pltpu.get_barrier_semaphore()
    greeted = [{axis: lax.rem(at[axis] + d, 4)} for axis in ("x", "y") for d in (1, 2, 3)] + [core]
    for where in greeted:
        pl.semaphore_signal(barrier, inc=1, device_id=where, device_id_type=MESH)

    def z_signal(sem, test, where):
        @pl.when(test)
        def _():
            pl.semaphore_signal(sem, inc=1, device_id=where, device_id_type=MESH)

    line = [lax.rem(zl + d, 4) for d in (1, 2, 3)]
    for z in line:
        z_signal(barrier, z > zl, {"zl": z})
    z_signal(barrier, zh == 0, partner)

    loads = {}

    def load(name, src, dst):
        copy = pltpu.make_async_copy(src, dst, load_sem.at[len(loads)])
        copy.start()
        loads[name] = copy

    load("f", f_hbm, f_v)
    load("p", p_hbm.at[pl.ds(aligned(zh * 2 + c, KF), KF), :], p_v)

    def columns(s, member, off, width):
        return pl.ds(pl.multiple_of(BASE[s] + member * CHUNK[s] + off, 128), width)

    def late_loads():
        for b in every:
            for s, off, width, seg in segs[b]:
                load(("g", b, s), g_hbm.at[:, columns(s, pos[RING[s]], off, width)], g_v.at[pl.ds(0, TOK), seg])
        here = {"zl": zl, "x": x, "y": y}
        for s, axis in enumerate(RING):
            for j, where in enumerate([{}] + [p[1] for p in peers[axis]]):
                w = here | where
                row = w["zl"] * 16 + w["x"] * 4 + w["y"]
                load(("p", s, j), p_hbm.at[pl.ds(aligned(row, ROWS), ROWS), :], pd_v.at[s, pl.ds(j * ROWS, ROWS), :])
        load("m", m_hbm, mom_v)

    grads = [group_of(g_v.at[pl.ds(TOK, 3 * TOK), lanes(b)]) for b in every]

    def grad_start(b):
        copies = []
        for j in range(3):
            for s, off, width, seg in segs[b]:
                to, where, slot = peers[RING[s]][j]
                copies.append((
                    g_hbm.at[:, columns(s, to, off, width)],
                    g_v.at[pl.ds(aligned(1 + slot, TOK), TOK), seg], where,
                ))
        start(grads[b], copies)

    def sum_send(b):
        arrive(f"got{b}", grads[b])
        for s, off, width, seg in segs[b]:
            loads["g", b, s].wait()
            panel[:, seg] = dot(mixed[s], g_v[:, seg])
            if C_TYPE != jnp.float32:
                panel_s[:, seg] = panel[:, seg].astype(C_TYPE)
        source = panel if C_TYPE == jnp.float32 else panel_s
        copies = []
        for j in range(3):
            for s, off, width, seg in segs[b]:
                to, where, slot = peers[CROSS[s]][j]
                copies.append((source.at[pl.ds(aligned(to, 64), 64), seg], crecv.at[slot, :, seg], where))
        return send(copies, crecv.at[:, :, lanes(b)])

    def reduce_send(b, group):
        arrive(f"C{b}", group)
        for s, off, width, seg in segs[b]:
            total = panel[pl.ds(aligned(pos[CROSS[s]], 64), 64), seg]
            for k in range(3):
                total = total + crecv[k, :, seg].astype(jnp.float32)
            quart[:, seg] = total
        copies = []
        for j in range(3):
            for s, off, width, seg in segs[b]:
                to, where, slot = peers[THIRD[s]][j]
                copies.append((quart.at[pl.ds(aligned(to, 16), 16), seg], drecv.at[slot, :, seg], where))
        return send(copies, drecv.at[:, :, lanes(b)])

    squares = []

    def gather_send(b, group):
        arrive(f"D{b}", group)
        places = {}
        for s, off, width, seg in segs[b]:
            total = quart[pl.ds(aligned(pos[THIRD[s]], 16), 16), seg]
            total = (total + drecv[2, :, seg]) + (drecv[0, :, seg] + drecv[1, :, seg])
            places[s] = pl.ds(pl.multiple_of(pos[CROSS[s]] * 64 + pos[THIRD[s]] * 16, 16), 16)
            full[places[s], seg] = total.astype(E_TYPE)
            squares.append(tile_squares(total))
        copies = []
        for j in range(3):
            for s, off, width, seg in segs[b]:
                piece = full.at[places[s], seg]
                copies.append((piece, piece, peers[THIRD[s]][j][1]))
        return send(copies, full.at[pl.ds(0, 48), lanes(b)])

    def cross_send(b, group):
        arrive(f"E{b}", group)
        copies = []
        for j in range(3):
            for s, off, width, seg in segs[b]:
                block = full.at[pl.ds(aligned(pos[CROSS[s]], 64), 64), seg]
                copies.append((block, block, peers[CROSS[s]][j][1]))
        return send(copies, full.at[pl.ds(0, 192), lanes(b)])

    def decode_send(b, group):
        arrive(f"F{b}", group)
        for s, off, width, seg in segs[b]:
            for j in range(4):
                if ("p", s, j) in loads:
                    loads.pop(("p", s, j)).wait()
            whole = full[:, seg]
            if E_TYPE == jnp.float32:
                high = whole.astype(jnp.bfloat16)
                low = (whole - high.astype(jnp.float32)).astype(jnp.bfloat16)
                rows = dot(pd_v[s], high) + dot(pd_v[s], low)
            else:
                rows = dot(pd_v[s], whole)
            panel[pl.ds(0, ROWS), seg] = rows[:ROWS]
            for j in range(3):
                dec_s[j, :, seg] = rows[(j + 1) * ROWS : (j + 2) * ROWS].astype(G_TYPE)
        copies = []
        for j in range(3):
            for s, off, width, seg in segs[b]:
                to, where, slot = peers[RING[s]][j]
                copies.append((dec_s.at[j, :, seg], dec_r.at[slot, :, seg], where))
        return send(copies, dec_r.at[:, :, lanes(b)])

    def spread(level, where):
        copies = [(sq.at[level, 0], sq.at[level, 1 + k], w) for k, w in enumerate(where)]
        return send(copies, sq.at[level, pl.ds(1, len(where))])

    def collect(level, group, n):
        arrive(f"sq{level}", group)
        total = sq[level, 0]
        for k in range(n):
            total = total + sq[level, 1 + k]
        sq[level + 1, 0] = total

    with scope("barrier"):
        pl.semaphore_wait(barrier, len(greeted) + zl + zh)
    grad_start(0)
    waits_long = zh * 4 + zl < AHEAD

    @pl.when(waits_long)
    def _():
        grad_start(1)

    for z in line:
        z_signal(ready.at[0], z < zl, {"zl": z})
    z_signal(ready.at[1], zh == 1, partner)
    mine = pl.ds(aligned(c, 128), 128)
    theirs = pl.ds(aligned(1 - c, 128), 128)
    with scope("mpart"):
        loads["f"].wait()
        loads["p"].wait()
        mpart[...] = dot(f_v[...], p_v[...])
    parts = [pl.ds(h * 128, 128) for h in BOTH]
    m1 = [send([(mpart.at[theirs, part], mrecv.at[0, :, part], core)], mrecv.at[0, :, part]) for part in parts]
    late_loads()
    m2 = []
    for h, part in enumerate(parts):
        arrive(f"m1{h}", m1[h])
        msum[:, part] = mpart[mine, part] + mrecv[0, :, part]
        if h == 0:

            @pl.when(zh == 0)
            def _():
                pl.semaphore_wait(ready.at[1], 1)

        m2.append(send([(msum.at[:, part], mrecv.at[1, :, part], partner)], msum.at[:, part]))

    @pl.when(zl < 3)
    def _():
        pl.semaphore_wait(ready.at[0], 3 - zl)


    def spot(s, part, slot):
        return mixed.at[s, part, pl.ds(pl.multiple_of((1 + slot) * TOK + c * 128, 128), 128)]

    direct, z_direct = {}, []
    passed = group_of(mixed.at[pl.ds(0, 2), :, pl.ds(0, 4 * 128)])
    z_passed = group_of(mixed.at[2, :, pl.ds(0, 4 * 128)])
    for h, part in enumerate(parts):
        arrive(f"m2{h}", m2[h])
        own = (msum[:, part] + mrecv[1, :, part]).T.astype(jnp.bfloat16)
        for s in range(3):
            mixed[s, part, mine] = own
        own = mixed.at[0, part, mine]
        for j in range(3):
            slot = peers["a"][j][2]
            direct[h, slot] = send(
                [(own, spot(s, part, slot), peers[RING[s]][j][1]) for s in BOTH],
                mixed.at[pl.ds(0, 2), part, pl.ds(0, 128)],
            )
        start(passed, [(mixed.at[s, part, mine], mixed.at[s, part, mine], core) for s in BOTH])
        start(z_passed, [(mixed.at[2, part, mine], mixed.at[2, part, mine], core)])
        z_direct.append(send(
            [(own, spot(2, part, slot), where) for _, where, slot in peers["z"]], mixed.at[2, part, pl.ds(0, 3 * 128)]
        ))

    grad_start(Z)

    @pl.when(jnp.logical_not(waits_long))
    def _():
        grad_start(1)

    for h, part in enumerate(parts):
        for slot in (0, 2, 1):
            arrive(f"direct{h}{slot}", direct[h, slot])
            start(passed, [(spot(s, part, slot), spot(1 - s, part, slot), core) for s in BOTH])
    arrive("passed", passed)
    moving = [sum_send(0), sum_send(1)]
    moving = [reduce_send(b, moving[b]) for b in BOTH]
    for h, part in enumerate(parts):
        arrive(f"z_direct{h}", z_direct[h])
        start(z_passed, [(spot(2, part, slot), spot(2, part, slot), core) for slot in range(3)])
    arrive("z_passed", z_passed)
    moving.append(sum_send(Z))
    moving[0] = gather_send(0, moving[0])
    moving[Z] = reduce_send(Z, moving[Z])
    moving[1] = gather_send(1, moving[1])
    moving[Z] = gather_send(Z, moving[Z])
    total = squares[0]
    for one in squares[1:]:
        total = total + one
    sq[0, 0] = total
    plane = [{"x": lax.rem(x + i, 4), "y": lax.rem(y + j, 4)} for i in range(4) for j in range(4) if i or j]
    q = spread(0, plane)
    moving = [cross_send(b, moving[b]) for b in every]
    collect(0, q, 15)
    stacked = [{"zl": z} for z in line] + [partner] + [{"zl": z} | partner for z in line]
    q = spread(1, [core] + [where | also for where in stacked for also in ({}, core)])
    final = {b: decode_send(b, moving[b]) for b in (0, Z, 1)}
    collect(1, q, 15)
    square_sum = jnp.sum(sq[2, 0], axis=(0, 1), keepdims=True)
    scale = 0.1 * (jnp.float32(math.sqrt(R * FF)) / jnp.sqrt(square_sum + 1e-06))

    loads["m"].wait()

    def finish(s, member, off, width, rows):
        cols = columns(s, member, off, width)
        out_ref[:, cols] = 0.9 * mom_v[:, cols] + scale * rows.astype(jnp.float32)

    for b in every:
        for s, off, width, seg in segs[b]:
            finish(s, pos[RING[s]], off, width, panel[pl.ds(0, ROWS), seg])
    for b in (0, Z, 1):
        arrive(f"fin{b}", final[b])
        for s, off, width, seg in segs[b]:
            for slot in range(3):
                finish(s, origin(RING[s], slot), off, width, dec_r[slot, :, seg])
    assert len(groups) == SEMS
    with scope("sendwait"):
        for group in groups:
            group.wait_send()


def local(features, projection, out_grad, momentum):
    dma = pltpu.SemaphoreType.DMA
    f32, bf16 = jnp.float32, jnp.bfloat16
    return pl.pallas_call(
        kernel,
        out_shape=jax.ShapeDtypeStruct((ROWS, COLS), f32),
        in_specs=[pl.BlockSpec(memory_space=pltpu.HBM)] * 4,
        out_specs=pl.BlockSpec(memory_space=pltpu.VMEM),
        scratch_shapes=[
            pltpu.VMEM((TOK, KF), bf16),
            pltpu.VMEM((KF, R), bf16),
            pltpu.VMEM((4 * TOK, LANES), bf16),
            pltpu.VMEM((ROWS, COLS), f32),
            pltpu.VMEM((3, 4 * ROWS, R), bf16),
            pltpu.VMEM((TOK, R), f32),
            pltpu.VMEM((2, 128, R), f32),
            pltpu.VMEM((128, R), f32),
            pltpu.VMEM((3, R, 4 * TOK), bf16),
            pltpu.VMEM((R, LANES), f32),
            pltpu.VMEM((R, LANES), C_TYPE),
            pltpu.VMEM((3, 64, LANES), C_TYPE),
            pltpu.VMEM((64, LANES), f32),
            pltpu.VMEM((3, 16, LANES), f32),
            pltpu.VMEM((R, LANES), E_TYPE),
            pltpu.VMEM((3, ROWS, LANES), G_TYPE),
            pltpu.VMEM((3, ROWS, LANES), G_TYPE),
            pltpu.VMEM((3, 16, 8, 128), f32),
            dma((20,)),
            dma((SEMS,)),
            dma((SEMS,)),
            pltpu.SemaphoreType.REGULAR((2,)),
        ],
        compiler_params=pltpu.CompilerParams(
            collective_id=0, has_side_effects=True, vmem_limit_bytes=40 * 1024 * 1024,
        ),
        name="flora",
    )(*[pltpu.with_memory_space_constraint(a, pltpu.HBM) for a in (features, projection, out_grad, momentum)])


def solution(mesh):
    finer = Mesh(mesh.devices.reshape(4, 4, 4, 2, 2), ("zl", "x", "y", "zh", "c"))
    return jax.shard_map(
        local,
        mesh=finer,
        in_specs=(P(DP, MP), P(), P(DP, MP), P(DP, MP)),
        out_specs=P(DP, MP),
        check_vma=False,
    )
```

time: 578 us -> 56.1 us (0.10)
  waiting for transfers between devices: 399 us -> 0 us
  blocking collectives: 113 us -> 0 us
  Pallas kernels: 0 us -> 54.6 us
  local copies, waits for them, and re-layouts: 17.7 us -> 1.39 us
  matrix products: 15.7 us -> 0 us
  between operations: 14.1 us -> 0.01 us
  other arithmetic: 8.07 us -> 0 us
    unnamed x3 -> x0, waiting for transfers between devices: 333 us -> none
    psum x5 -> x0, blocking collectives: 113 us -> none  [over_axes(): shard = lax.psum(shard, axis)]
    all_gather x1 -> x0, waiting for transfers between devices: 66.8 us -> none  [local(): lax.all_gather(features, MP, axis=1, tiled=True)]
    pallas_call x0 -> x1, Pallas kernels: none -> 54.6 us  [local(): pl.pallas_call(kernel, out_shape=jax.ShapeDtypeStruct((ROWS, COLS), f32),...]
    dot_general x2 -> x0, matrix products: 15.7 us -> none  [the longest x1 8.76 us: local(): lax.dot_general(out_grad, mixed_rows, (((0,), (0,)), ((), ())), preferred...]
    all_to_all x2 -> x0, local copies, waits for them, and re-layouts: 8.55 us -> none  [local(): lax.all_to_all(strip_cols, DP, split_axis=0, concat_axis=1, tiled=True)]
  transfers between devices with their start and end apart: 3 -> 0, of which waited for: 2 -> 0; matrix products, arithmetic and copies ran while one was open for 0% -> 0% of each run, Pallas kernels for 0% -> 0%
where the time goes in v3:
time: 56.1 us; the launch traced here: 56 us
  Pallas kernels  54.6 us (97%)
  local copies, waits for them, and re-layouts  1.39 us (2%)
    pallas_call x1, Pallas kernels, local(): pl.pallas_call(kernel, out_shape=jax.ShapeDtypeStruct((ROWS, COLS), f32),...  54.6 us
    unnamed x1, local copies, waits for them, and re-layouts  1.39 us

profile of v3, /device:TPU:1, one launch (start us, length us, event | category | flops | bytes accessed | tf_op | source)
XLA Modules:
  0.0 56.0 jit_solution(7095130516851219112)
XLA Ops:
  0.0 54.6 %flora.1 = f32[112,5120]{1,0:T(8,128)S(1)} custom-call(bf16[256,1792]{1,0:T(8,128)(2,1)} %f_hbm.1, bf16[7168,256]{1,0:T(8,128)(2,1)} %p_hbm.1, bf16[256,5120]{1,0:T(8,128)(2,1)} %g_hbm.1, f32[112,5120]{1,0:T(8,128)} %m_hbm.1), custom_call_target="tpu_custom_call" | custom-call | tf_op jit(solution)/shard_map/flora/pallas_call | solution.py:387
  54.6 1.4 %copy.6 = f32[112,5120]{1,0:T(8,128)} copy(f32[112,5120]{1,0:T(8,128)S(1)} %flora.1) | data formatting | bytes 4587520

commit v4 on v3

--- a/solution.py
+++ b/solution.py
@@ -262,26 +262,26 @@
             total = total + sq[level, 1 + k]
         sq[level + 1, 0] = total
 
-    with scope("barrier"):
-        pl.semaphore_wait(barrier, len(greeted) + zl + zh)
-    grad_start(0)
-    waits_long = zh * 4 + zl < AHEAD
-
-    @pl.when(waits_long)
-    def _():
-        grad_start(1)
-
-    for z in line:
-        z_signal(ready.at[0], z < zl, {"zl": z})
-    z_signal(ready.at[1], zh == 1, partner)
-    mine = pl.ds(aligned(c, 128), 128)
-    theirs = pl.ds(aligned(1 - c, 128), 128)
     with scope("mpart"):
         loads["f"].wait()
         loads["p"].wait()
         mpart[...] = dot(f_v[...], p_v[...])
+    mine = pl.ds(aligned(c, 128), 128)
+    theirs = pl.ds(aligned(1 - c, 128), 128)
     parts = [pl.ds(h * 128, 128) for h in BOTH]
+    with scope("barrier"):
+        pl.semaphore_wait(barrier, len(greeted) + zl + zh)
     m1 = [send([(mpart.at[theirs, part], mrecv.at[0, :, part], core)], mrecv.at[0, :, part]) for part in parts]
+    grad_start(0)
+    waits_long = zh * 4 + zl < AHEAD
+
+    @pl.when(waits_long)
+    def _():
+        grad_start(1)
+
+    for z in line:
+        z_signal(ready.at[0], z < zl, {"zl": z})
+    z_signal(ready.at[1], zh == 1, partner)
     late_loads()
     m2 = []
     for h, part in enumerate(parts):
@@ -349,14 +349,14 @@
     total = squares[0]
     for one in squares[1:]:
         total = total + one
-    sq[0, 0] = total
+    sq[0, 0] = jnp.sum(total, axis=0, keepdims=True)
     plane = [{"x": lax.rem(x + i, 4), "y": lax.rem(y + j, 4)} for i in range(4) for j in range(4) if i or j]
     q = spread(0, plane)
     moving = [cross_send(b, moving[b]) for b in every]
     collect(0, q, 15)
     stacked = [{"zl": z} for z in line] + [partner] + [{"zl": z} | partner for z in line]
     q = spread(1, [core] + [where | also for where in stacked for also in ({}, core)])
-    final = {b: decode_send(b, moving[b]) for b in (0, Z, 1)}
+    final = {b: decode_send(b, moving[b]) for b in every}
     collect(1, q, 15)
     square_sum = jnp.sum(sq[2, 0], axis=(0, 1), keepdims=True)
     scale = 0.1 * (jnp.float32(math.sqrt(R * FF)) / jnp.sqrt(square_sum + 1e-06))
@@ -370,7 +370,7 @@
     for b in every:
         for s, off, width, seg in segs[b]:
             finish(s, pos[RING[s]], off, width, panel[pl.ds(0, ROWS), seg])
-    for b in (0, Z, 1):
+    for b in every:
         arrive(f"fin{b}", final[b])
         for s, off, width, seg in segs[b]:
             for slot in range(3):
@@ -407,7 +407,7 @@
             pltpu.VMEM((R, LANES), E_TYPE),
             pltpu.VMEM((3, ROWS, LANES), G_TYPE),
             pltpu.VMEM((3, ROWS, LANES), G_TYPE),
-            pltpu.VMEM((3, 16, 8, 128), f32),
+            pltpu.VMEM((3, 16, 1, 128), f32),
             dma((20,)),
             dma((SEMS,)),
             dma((SEMS,)),

time: 56.1 us -> 54.6 us (0.973)
  Pallas kernels: 54.6 us -> 53.1 us
    pallas_call x1, Pallas kernels: 54.6 us -> 53.1 us  [local(): pl.pallas_call(kernel, out_shape=jax.ShapeDtypeStruct((ROWS, COLS), f32),...]
where the time goes in v4:
time: 54.6 us; the launch traced here: 54.5 us
  Pallas kernels  53.1 us (97%)
  local copies, waits for them, and re-layouts  1.39 us (3%)
    pallas_call x1, Pallas kernels, local(): pl.pallas_call(kernel, out_shape=jax.ShapeDtypeStruct((ROWS, COLS), f32),...  53.1 us
    unnamed x1, local copies, waits for them, and re-layouts  1.39 us

profile of v4, /device:TPU:1, one launch (start us, length us, event | category | flops | bytes accessed | tf_op | source)
XLA Modules:
  0.0 54.5 jit_solution(11560055238102492212)
XLA Ops:
  0.0 53.1 %flora.1 = f32[112,5120]{1,0:T(8,128)S(1)} custom-call(bf16[256,1792]{1,0:T(8,128)(2,1)} %f_hbm.1, bf16[7168,256]{1,0:T(8,128)(2,1)} %p_hbm.1, bf16[256,5120]{1,0:T(8,128)(2,1)} %g_hbm.1, f32[112,5120]{1,0:T(8,128)} %m_hbm.1), custom_call_target="tpu_custom_call" | custom-call | tf_op jit(solution)/shard_map/flora/pallas_call | solution.py:387
  53.1 1.4 %copy.6 = f32[112,5120]{1,0:T(8,128)} copy(f32[112,5120]{1,0:T(8,128)S(1)} %flora.1) | data formatting | bytes 4587520

commit v5 on v4

--- a/solution.py
+++ b/solution.py
@@ -174,18 +174,18 @@
 
     def sum_send(b):
         arrive(f"got{b}", grads[b])
+        group = group_of(crecv.at[:, :, lanes(b)])
         for s, off, width, seg in segs[b]:
             loads["g", b, s].wait()
             panel[:, seg] = dot(mixed[s], g_v[:, seg])
             if C_TYPE != jnp.float32:
                 panel_s[:, seg] = panel[:, seg].astype(C_TYPE)
-        source = panel if C_TYPE == jnp.float32 else panel_s
-        copies = []
-        for j in range(3):
-            for s, off, width, seg in segs[b]:
-                to, where, slot = peers[CROSS[s]][j]
-                copies.append((source.at[pl.ds(aligned(to, 64), 64), seg], crecv.at[slot, :, seg], where))
-        return send(copies, crecv.at[:, :, lanes(b)])
+            source = panel if C_TYPE == jnp.float32 else panel_s
+            start(group, [
+                (source.at[pl.ds(aligned(to, 64), 64), seg], crecv.at[slot, :, seg], where)
+                for to, where, slot in peers[CROSS[s]]
+            ])
+        return group
 
     def reduce_send(b, group):
         arrive(f"C{b}", group)
@@ -230,6 +230,7 @@
 
     def decode_send(b, group):
         arrive(f"F{b}", group)
+        out = group_of(dec_r.at[:, :, lanes(b)])
         for s, off, width, seg in segs[b]:
             for j in range(4):
                 if ("p", s, j) in loads:
@@ -244,12 +245,11 @@
             panel[pl.ds(0, ROWS), seg] = rows[:ROWS]
             for j in range(3):
                 dec_s[j, :, seg] = rows[(j + 1) * ROWS : (j + 2) * ROWS].astype(G_TYPE)
-        copies = []
-        for j in range(3):
-            for s, off, width, seg in segs[b]:
-                to, where, slot = peers[RING[s]][j]
-                copies.append((dec_s.at[j, :, seg], dec_r.at[slot, :, seg], where))
-        return send(copies, dec_r.at[:, :, lanes(b)])
+            start(out, [
+                (dec_s.at[j, :, seg], dec_r.at[slot, :, seg], where)
+                for j, (_, where, slot) in enumerate(peers[RING[s]])
+            ])
+        return out
 
     def spread(level, where):
         copies = [(sq.at[level, 0], sq.at[level, 1 + k], w) for k, w in enumerate(where)]
@@ -336,10 +336,10 @@
             start(passed, [(spot(s, part, slot), spot(1 - s, part, slot), core) for s in BOTH])
     arrive("passed", passed)
     moving = [sum_send(0), sum_send(1)]
-    moving = [reduce_send(b, moving[b]) for b in BOTH]
     for h, part in enumerate(parts):
         arrive(f"z_direct{h}", z_direct[h])
         start(z_passed, [(spot(2, part, slot), spot(2, part, slot), core) for slot in range(3)])
+    moving = [reduce_send(b, moving[b]) for b in BOTH]
     arrive("z_passed", z_passed)
     moving.append(sum_send(Z))
     moving[0] = gather_send(0, moving[0])

time: 54.6 us -> 54.8 us (level)
  no operation moved by 1% of the time
where the time goes in v5:
time: 54.8 us; the launch traced here: 54.7 us
  Pallas kernels  53.3 us (97%)
  local copies, waits for them, and re-layouts  1.39 us (3%)
    pallas_call x1, Pallas kernels, local(): pl.pallas_call(kernel, out_shape=jax.ShapeDtypeStruct((ROWS, COLS), f32),...  53.3 us
    unnamed x1, local copies, waits for them, and re-layouts  1.39 us

profile of v5, /device:TPU:1, one launch (start us, length us, event | category | flops | bytes accessed | tf_op | source)
XLA Modules:
  0.0 54.7 jit_solution(15203894936779914738)
XLA Ops:
  0.0 53.3 %flora.1 = f32[112,5120]{1,0:T(8,128)S(1)} custom-call(bf16[256,1792]{1,0:T(8,128)(2,1)} %f_hbm.1, bf16[7168,256]{1,0:T(8,128)(2,1)} %p_hbm.1, bf16[256,5120]{1,0:T(8,128)(2,1)} %g_hbm.1, f32[112,5120]{1,0:T(8,128)} %m_hbm.1), custom_call_target="tpu_custom_call" | custom-call | tf_op jit(solution)/shard_map/flora/pallas_call | solution.py:387
  53.3 1.4 %copy.6 = f32[112,5120]{1,0:T(8,128)} copy(f32[112,5120]{1,0:T(8,128)S(1)} %flora.1) | data formatting | bytes 4587520
